TPU v7x, 32 devices: a whole 2x2x4 slice. The times are simulated.
32 devices in a mesh: gx: 4 (over y, core), gy: 8 (over z, x).
Axes of the slice: x: 2, y: 2, z: 4, core: 2. Of those that a mesh axis runs over, the one named last changes fastest.
Arguments:
- pool_old: float32 [40, 131072], P(None, ('gx', 'gy')), may hold values from 0.5 to 2
- pool_new: float32 [40, 131072], P(None, ('gx', 'gy')), may hold values from 0.5 to 2
- flux: float32 [40, 131072], P(None, ('gx', 'gy')), may hold values from -6 to 6
- area: float32 [131072], P(('gx', 'gy')), may hold values from 0.05 to 1
- pft_id: int32 [131072], P(('gx', 'gy')), may hold values from 0 to 78
- region_id: int32 [131072], P(('gx', 'gy')), may hold values from 0 to 31, as said below
Outputs:
- pool_totals: float32 [40, 2528], replicated
- error_totals: float32 [40, 2528], replicated
Inputs may be any that keep to these rules, and one draw needn't show every extreme that they name: `region_id`: patch i lies in block k = i // 4096; with K = 32 blocks, its region is (k * 32) // K or ((k * 32) // K + 1) mod 32.
All inputs are finite; a program needn't handle non-finite values.
Results may differ from a plain program's by a relative error of at most 0.000076.
Values sent between devices are 32-bit elements; how exact they have to be, the bound alone decides.
A program may use at most 64 MiB of HBM per device.

v0:
```python
import jax
import jax.numpy as jnp
from jax import lax
from jax.sharding import PartitionSpec as P

POOLS = 40
PFT = 79
REGION = 32
CELLS = 2528


def shards(pool_old, pool_new, flux, area, pft_id, region_id):
    width_x = lax.axis_size("gx")
    width_y = lax.axis_size("gy")
    devices_all = width_x * width_y
    position = lax.axis_index("gx") * width_y + lax.axis_index("gy")
    base = position * REGION // devices_all
    offset_here = (region_id - base) % REGION
    compact_cell = pft_id * 2 + offset_here
    stored = area[None, :] * pool_new
    balance = area[None, :] * (pool_new - pool_old - 0.5 * flux)
    stacked = jnp.concatenate([stored, balance], axis=0)
    rows = stacked.shape[0]
    patch_count = stacked.shape[1]
    block = min(512, patch_count)
    blocks = patch_count // block
    stacked_blocks = stacked.reshape(rows, blocks, block).transpose(1, 0, 2)
    cell_blocks = compact_cell.reshape(blocks, block)
    columns = jnp.arange(2 * PFT, dtype=jnp.int32)

    def accumulate(totals, inputs):
        values, cells_here = inputs
        onehot = (cells_here[:, None] == columns[None, :]).astype(jnp.float32)
        added = jnp.dot(
            values, onehot, preferred_element_type=jnp.float32, precision=lax.Precision.HIGHEST
        )
        return (totals + added, None)

    local_table, _ = lax.scan(
        accumulate, jnp.zeros((rows, 2 * PFT), jnp.float32), (stacked_blocks, cell_blocks)
    )
    local_table = local_table.reshape(rows, PFT, 2)
    region_axis = jnp.arange(REGION, dtype=jnp.int32)
    pair_axis = jnp.arange(2, dtype=jnp.int32)
    span = REGION // width_x + 1
    start = lax.axis_index("gx") * (REGION // width_x)
    span_axis = jnp.arange(span, dtype=jnp.int32)
    into_group = ((base - start + pair_axis)[:, None] == span_axis[None, :]).astype(jnp.float32)
    group_table = jnp.einsum(
        "apj,jw->apw", local_table, into_group, precision=lax.Precision.HIGHEST
    )
    group_total = lax.psum(group_table, "gy")
    into_full = (((start + span_axis) % REGION)[:, None] == region_axis[None, :]).astype(
        jnp.float32
    )
    placed = jnp.einsum("apw,wr->apr", group_total, into_full, precision=lax.Precision.HIGHEST)
    totals = lax.psum(placed.reshape(rows, CELLS), "gx")
    patch_all = patch_count * devices_all
    totals = totals * jnp.float32(CELLS / patch_all)
    return (totals[:POOLS], totals[POOLS:])


def solution(mesh):
    return jax.shard_map(
        shards,
        mesh=mesh,
        in_specs=(
            P(None, ("gx", "gy")),
            P(None, ("gx", "gy")),
            P(None, ("gx", "gy")),
            P(("gx", "gy")),
            P(("gx", "gy")),
            P(("gx", "gy")),
        ),
        out_specs=(P(), P()),
        check_vma=False,
    )
```

profile of v0, /device:TPU:0, one launch (start us, length us, event | category | flops | bytes accessed | tf_op | source)
XLA Modules:
  0.0 140.4 jit_solution(4403642553132659175)
XLA Ops:
  7.2 0.0 all-reduce.3.cloned.1.call-start
  7.2 0.8 fusion.4
  8.0 1.6 %broadcast_multiply_fusion.1 = (f32[40,4096]{1,0:T(8,128)S(1)}, f32[40,4096]{1,0:T(8,128)S(1)}) fusion(f32[40,4096]{1,0:T(8,128)} %param.9, f32[4096]{0:T(1024)} %param.11, f32[40,4096]{1,0:T(8,128)} %param.10, f32[40,4096]{1,0:T(8,128)} %param.8), kind=kLoop, calls=%fused_computation.10 | loop fusion | flops 819200 | bytes 3293184 | tf_op jit(solution)/shard_map/mul | solution.py:20
  9.6 0.1 pad_maximum_fusion
  9.7 0.8 copy.13
  10.6 4.8 %while.11 = (s32[]{:T(128)}, f32[80,158]{1,0:T(8,128)S(1)}, f32[8,80,512]{2,0,1:T(8,128)S(1)}, s32[8,512]{1,0:T(8,128)S(1)}, s32[]{:T(128)}, /*index=5*/s32[]{:T(128)}) while((s32[]{:T(128)}, f32[80,158]{1,0:T(8,128)S(1)}, f32[8,80,512]{2,0,1:T(8,128)S(1)}, s32[8,512]{1,0:T(8,128)S(1)}, s32[]{:T(128)}, /*index=5*/s32[]{:T(128)}) %tuple.36), condition=%wide.region_1.2_spmd.clone, body=%wide.region_0.1_spmd.clone.sunk | while | flops 77766336 | bytes 598871 | solution.py:39
  10.6 0.1 constant_dynamic-slice_fusion.5
  10.8 0.4 convolution_add_fusion.2
  11.2 0.1 constant_dynamic-slice_fusion.5
  11.4 0.4 convolution_add_fusion.2
  11.8 0.1 constant_dynamic-slice_fusion.5
  12.0 0.4 convolution_add_fusion.2
  12.4 0.1 constant_dynamic-slice_fusion.5
  12.5 0.4 convolution_add_fusion.2
  13.0 0.1 constant_dynamic-slice_fusion.5
  13.1 0.4 convolution_add_fusion.2
  13.6 0.1 constant_dynamic-slice_fusion.5
  13.7 0.4 convolution_add_fusion.2
  14.2 0.1 constant_dynamic-slice_fusion.5
  14.3 0.4 convolution_add_fusion.2
  14.8 0.1 constant_dynamic-slice_fusion.5
  14.9 0.4 convolution_add_fusion.2
  15.3 0.1 copy.10
  15.5 1.4 fusion.9
  16.9 0.0 all-reduce.3.cloned.1.call-update
  16.9 0.0 all-reduce.5.cloned.1.call-start
  17.0 76.4 %all-reduce.3.cloned.1.call-done = f32[80,79,9]{0,2,1:T(8,128)} async-done(((f32[80,79,9]{0,2,1:T(8,128)}), f32[80,79,9]{0,2,1:T(8,128)}) %all-reduce.3.cloned.1.call-update) | async-done | bytes 227536 | tf_op jit(solution)/shard_map/psum | solution.py:52
  93.4 1.9 %fusion.6 = f32[80,79,32]{0,2,1:T(8,128)S(1)} fusion(f32[80,79,9]{0,2,1:T(8,128)} %all-reduce.3.cloned.1.call-done, s32[9]{0:T(128)S(1)} %and_select_fusion), kind=kOutput, calls=%fused_computation.18 | convolution fusion | flops 21842208 | bytes 1036516 | tf_op jit(solution)/shard_map/apw,wr->apr/dot_general | solution.py:56
  95.3 1.3 copy.11
  96.6 0.0 all-reduce.5.cloned.1.call-update
  96.6 34.8 %all-reduce.5.cloned.1.call-done = f32[80,2528]{1,0:T(8,128)} async-done(((f32[80,2528]{1,0:T(8,128)}), f32[80,2528]{1,0:T(8,128)}) %all-reduce.5.cloned.1.call-update) | async-done | bytes 808976 | tf_op jit(solution)/shard_map/psum | solution.py:57
  131.4 1.2 broadcast_multiply_fusion
  132.7 0.9 fusion.15
  (13 shorter events, 0.2 us)
Async XLA Ops:
  7.2 86.3 %all-reduce.3.cloned.1.call-start = ((), (), s32[]{:S(2)}) async-start(), calls=%async_computation | async-start | bytes 1294336 | tf_op jit(solution)/shard_map/psum | solution.py:52
  16.9 114.5 %all-reduce.5.cloned.1.call-start = ((), (), s32[]{:S(2)}) async-start(), calls=%async_computation.1 | async-start | bytes 1638400 | tf_op jit(solution)/shard_map/psum | solution.py:57
Sparse Core Ops, SparseCore 0:
  17.0 76.3 all-reduce.2
  96.7 34.6 all-reduce.4
where the time goes:
time: 141 us; the launch traced here: 140 us
  waiting for transfers between devices  111 us (79%)
  between operations  14.1 us (10%)
  matrix products  6.42 us (5%)
  local copies, waits for them, and re-layouts  4.48 us (3%)
  other arithmetic  3.68 us (3%)
    psum x1, waiting for transfers between devices, shards(): group_total = lax.psum(group_table, 'gy')  76.4 us
    psum x1, waiting for transfers between devices, shards(): totals = lax.psum(placed.reshape(rows, CELLS), 'gx')  34.8 us
    dot_general x8, matrix products, accumulate(): jnp.dot(values, onehot, preferred_element_type=jnp.float32, precision=lax...  3.17 us
  transfers between devices with their start and end apart: 2, of which 2 were waited for; matrix products, arithmetic and copies ran while one was open for 0% of the time, Pallas kernels for 0%

commit v1 on v0

--- a/solution.py
+++ b/solution.py
@@ -49,7 +49,8 @@
     group_table = jnp.einsum(
         "apj,jw->apw", local_table, into_group, precision=lax.Precision.HIGHEST
     )
-    group_total = lax.psum(group_table, "gy")
+    pieces = lax.all_gather(group_table, "gy", axis=0, tiled=False)
+    group_total = pieces.sum(axis=0)
     into_full = (((start + span_axis) % REGION)[:, None] == region_axis[None, :]).astype(
         jnp.float32
     )

time: 141 us -> 126 us (0.89)
  waiting for transfers between devices: 111 us -> 94.8 us
  other arithmetic: 3.68 us -> 5.75 us
  matrix products: 6.42 us -> 4.51 us
    psum x1 -> x0, waiting for transfers between devices: 76.4 us -> none  [shards(): group_total = lax.psum(group_table, 'gy')]
    all_gather x0 -> x1, waiting for transfers between devices: none -> 60.7 us  [shards(): pieces = lax.all_gather(group_table, 'gy', axis=0, tiled=False)]
    reduce_sum x0 -> x1, other arithmetic: none -> 2.07 us  [shards(): group_total = pieces.sum(axis=0)]
where the time goes in v1:
time: 126 us; the launch traced here: 125 us
  waiting for transfers between devices  94.8 us (75%)
  between operations  14.2 us (11%)
  local copies, waits for them, and re-layouts  5.81 us (5%)
  other arithmetic  5.75 us (5%)
  matrix products  4.51 us (4%)
    all_gather x1, waiting for transfers between devices, shards(): pieces = lax.all_gather(group_table, 'gy', axis=0, tiled=False)  60.7 us
    psum x1, waiting for transfers between devices, shards(): totals = lax.psum(placed.reshape(rows, CELLS), 'gx')  34 us
    dot_general x8, matrix products, accumulate(): jnp.dot(values, onehot, preferred_element_type=jnp.float32, precision=lax...  3.17 us
  transfers between devices with their start and end apart: 2, of which 2 were waited for; matrix products, arithmetic and copies ran while one was open for 0% of the time, Pallas kernels for 0%

profile of v1, /device:TPU:0, one launch (start us, length us, event | category | flops | bytes accessed | tf_op | source)
XLA Modules:
  0.0 125.4 jit_solution(14067169427104414805)
XLA Ops:
  7.2 0.0 all-gather.3.cloned.1.call-start
  7.3 0.8 fusion.4
  8.0 1.6 %broadcast_multiply_fusion.1 = (f32[40,4096]{1,0:T(8,128)S(1)}, f32[40,4096]{1,0:T(8,128)S(1)}) fusion(f32[40,4096]{1,0:T(8,128)} %param.9, f32[4096]{0:T(1024)} %param.11, f32[40,4096]{1,0:T(8,128)} %param.10, f32[40,4096]{1,0:T(8,128)} %param.8), kind=kLoop, calls=%fused_computation.10 | loop fusion | flops 819200 | bytes 3293184 | tf_op jit(solution)/shard_map/mul | solution.py:20
  9.6 0.1 pad_maximum_fusion
  9.7 0.8 copy.24
  10.6 4.7 %while.11 = (s32[]{:T(128)}, f32[80,158]{1,0:T(8,128)S(1)}, f32[8,80,512]{2,0,1:T(8,128)S(1)}, s32[8,512]{1,0:T(8,128)S(1)}, s32[]{:T(128)}, /*index=5*/s32[]{:T(128)}) while((s32[]{:T(128)}, f32[80,158]{1,0:T(8,128)S(1)}, f32[8,80,512]{2,0,1:T(8,128)S(1)}, s32[8,512]{1,0:T(8,128)S(1)}, s32[]{:T(128)}, /*index=5*/s32[]{:T(128)}) %tuple.37), condition=%wide.region_1.2_spmd.clone, body=%wide.region_0.1_spmd.clone.sunk | while | flops 77766336 | bytes 598879 | solution.py:39
  10.6 0.1 constant_dynamic-slice_fusion.5
  10.8 0.4 convolution_add_fusion.2
  11.2 0.1 constant_dynamic-slice_fusion.5
  11.4 0.4 convolution_add_fusion.2
  11.8 0.1 constant_dynamic-slice_fusion.5
  12.0 0.4 convolution_add_fusion.2
  12.4 0.1 constant_dynamic-slice_fusion.5
  12.5 0.4 convolution_add_fusion.2
  13.0 0.1 constant_dynamic-slice_fusion.5
  13.1 0.4 convolution_add_fusion.2
  13.6 0.1 constant_dynamic-slice_fusion.5
  13.7 0.4 convolution_add_fusion.2
  14.2 0.1 constant_dynamic-slice_fusion.5
  14.3 0.4 convolution_add_fusion.2
  14.8 0.1 constant_dynamic-slice_fusion.5
  14.9 0.4 convolution_add_fusion.2
  15.3 0.1 copy.15
  15.5 0.5 fusion.9
  16.0 1.0 copy.16
  17.0 0.0 all-gather.3.cloned.1.call-update
  17.0 0.0 all-reduce.2.cloned.1.call-start
  17.1 60.7 %all-gather.3.cloned.1.call-done = f32[640,79,9]{1,0,2:T(8,128)} async-done(((f32[80,79,9]{1,0,2:T(8,128)}), f32[640,79,9]{1,0,2:T(8,128)}) %all-gather.3.cloned.1.call-update) | async-done | bytes 1820176 | tf_op jit(solution)/shard_map/all_gather | solution.py:52
  77.8 2.1 %reduce_sum.9 = f32[80,79,9]{1,0,2:T(8,128)S(1)} reduce(f32[8,80,79,9]{2,1,0,3:T(8,128)} %bitcast.27, f32[]{:T(128)} %constant.53.clone.1), dimensions={0}, to_apply=%region_2.3 | reduce | flops 398160 | bytes 2047684 | tf_op jit(solution)/shard_map/reduce_sum | solution.py:53
  79.9 0.4 copy.18
  80.3 0.8 fusion.6
  81.1 1.3 %copy.19 = f32[80,2528]{1,0:T(8,128)} copy(f32[80,2528]{0,1:T(8,128)S(1)} %bitcast.25) | data formatting | bytes 1617920 | tf_op jit(solution)/shard_map/reshape | solution.py:58
  82.4 0.0 all-reduce.2.cloned.1.call-update
  82.4 34.0 %all-reduce.2.cloned.1.call-done = f32[80,2528]{1,0:T(8,128)} async-done(((f32[80,2528]{1,0:T(8,128)}), f32[80,2528]{1,0:T(8,128)}) %all-reduce.2.cloned.1.call-update) | async-done | bytes 808976 | tf_op jit(solution)/shard_map/psum | solution.py:58
  116.4 1.2 broadcast_multiply_fusion
  117.6 0.9 fusion.15
  (13 shorter events, 0.1 us)
Async XLA Ops:
  7.2 70.7 %all-gather.3.cloned.1.call-start = ((), (), s32[]{:S(2)}) async-start(), calls=%async_computation.1 | async-start | bytes 3317760 | tf_op jit(solution)/shard_map/all_gather | solution.py:52
  17.0 99.4 %all-reduce.2.cloned.1.call-start = ((), (), s32[]{:S(2)}) async-start(), calls=%async_computation | async-start | bytes 1638400 | tf_op jit(solution)/shard_map/psum | solution.py:58
Sparse Core Ops, SparseCore 0:
  17.1 60.6 all-gather.2
  82.5 33.8 all-reduce.1
